TPU v7x, 32 devices: a whole 2x2x4 slice. The times are simulated.
32 devices in a mesh: tp: 2 (over x), dp: 4 (over y, core), rep: 4 (over z).
Axes of the slice: x: 2, y: 2, z: 4, core: 2. Of those that a mesh axis runs over, the one named last changes fastest.
Arguments:
- prompts: bfloat16 [12288, 8192], P(('dp', 'rep'), 'tp'), may hold values from -6 to 6
- frozen_projection_weight: bfloat16 [2, 8192, 2048], P(None, ('dp', 'rep'), 'tp'), may hold values from -5 to 5
- lowrank_down_factor: bfloat16 [2, 8192, 64], P(None, ('dp', 'rep')), may hold values from -0.119628906 to 0.119628906
- lowrank_up_factor: bfloat16 [2, 64, 2048], P(None, None, 'tp'), may hold values from -0.59765625 to 0.59765625
- magnitude: float32 [2, 2048], P(None, 'tp'), may hold values from 0.5 to 2
Outputs:
- key_values: bfloat16 [2, 12288, 2048], P(None, ('dp', 'rep'), 'tp')
All inputs are finite; a program needn't handle non-finite values.
Results may differ from a plain program's by a relative error of at most 0.0049.
Values may be sent and summed in bfloat16 or wider, within the bound.
A program may use at most 128 MiB of HBM per device.

v0:
```python
import jax
import jax.numpy as jnp
from jax import lax
from jax.sharding import PartitionSpec as P

epsilon = 1e-06


def combine_weight_rows(weight_rows, down_rows, up_matrix):
    return weight_rows.astype(jnp.float32) + jnp.dot(
        down_rows, up_matrix, preferred_element_type=jnp.float32
    )


def prefilled_shard_values(
    frozen_projection_weight, lowrank_down_factor, lowrank_up_factor, magnitude, current_layer_index
):
    combined_weight = combine_weight_rows(
        frozen_projection_weight[current_layer_index],
        lowrank_down_factor[current_layer_index],
        lowrank_up_factor[current_layer_index],
    )
    squares = lax.psum(jnp.sum(combined_weight * combined_weight, axis=0), ("dp", "rep"))
    factor = magnitude[current_layer_index] / jnp.sqrt(squares + epsilon)
    return (combined_weight * factor).astype(jnp.bfloat16)


def local(prompts, frozen_projection_weight, lowrank_down_factor, lowrank_up_factor, magnitude):
    layer_total = frozen_projection_weight.shape[0]
    features = lax.all_gather(prompts, "tp", axis=1, tiled=True)
    outputs = []
    for current_layer_index in range(layer_total):
        prefilled_key_values = prefilled_shard_values(
            frozen_projection_weight,
            lowrank_down_factor,
            lowrank_up_factor,
            magnitude,
            current_layer_index,
        )
        result = jnp.dot(
            features,
            lax.all_gather(prefilled_key_values, ("dp", "rep"), axis=0, tiled=True),
            preferred_element_type=jnp.float32,
        )
        outputs.append(result.astype(jnp.bfloat16))
    return jnp.stack(outputs)


def solution(mesh):
    in_specs = (
        P(("dp", "rep"), "tp"),
        P(None, ("dp", "rep"), "tp"),
        P(None, ("dp", "rep"), None),
        P(None, None, "tp"),
        P(None, "tp"),
    )
    out_specs = P(None, ("dp", "rep"), "tp")
    return jax.shard_map(local, mesh=mesh, in_specs=in_specs, out_specs=out_specs, check_vma=False)
```

profile of v0, /device:TPU:0, one launch (start us, length us, event | category | flops | bytes accessed | tf_op | source)
XLA Modules:
  0.0 448.4 jit_solution(12562199270056117100)
XLA Ops:
  6.5 0.0 copy-start.2
  6.5 0.0 copy-start.3
  6.5 0.0 all-gather.6.cloned.1.call-start
  6.5 0.7 all-gather.6.cloned.1.call-update
  7.3 0.0 all-gather.4.cloned.1.call-start
  7.3 0.2 copy-done.2
  7.5 0.0 copy-done.3
  7.5 0.0 copy-start
  7.5 1.8 multiply_reduce_fusion
  9.4 0.1 copy-done
  9.4 0.0 copy-start.4
  9.4 1.8 multiply_reduce_fusion.1
  11.2 35.9 %all-reduce = (f32[1024]{0:T(1024)S(1)}, f32[1024]{0:T(1024)S(1)}) all-reduce(f32[1024]{0:T(1024)S(1)} %get-tuple-element.9, f32[1024]{0:T(1024)S(1)} %get-tuple-element.11), channel_id=1, replica_groups=mesh['tp'=2,'dp'=4,'rep'=4] {'dp','rep'}, use_global_device_ids=true, to_apply=%region_3.0 | all-reduce | flops 2048 | bytes 16384 | tf_op jit(solution)/shard_map/psum | solution.py:23
  47.2 0.0 copy-done.4
  47.2 2.8 multiply_convert_fusion.1
  50.0 0.0 all-gather.4.cloned.1.call-update
  50.1 0.0 all-gather.8.cloned.1.call-start
  50.1 1.2 multiply_convert_fusion
  51.4 0.0 all-gather.8.cloned.1.call-update
  51.4 112.8 %all-gather.6.cloned.1.call-done = bf16[768,8192]{1,0:T(8,128)(2,1)} async-done(((bf16[768,4096]{1,0:T(8,128)(2,1)}), bf16[768,8192]{1,0:T(8,128)(2,1)}) %all-gather.6.cloned.1.call-update) | async-done | bytes 12582928 | tf_op jit(solution)/shard_map/all_gather | solution.py:30
  164.1 128.7 %all-gather.4.cloned.1.call-done = bf16[8192,1024]{1,0:T(8,128)(2,1)} async-done(((bf16[512,1024]{1,0:T(8,128)(2,1)}), bf16[8192,1024]{1,0:T(8,128)(2,1)}) %all-gather.4.cloned.1.call-update) | async-done | bytes 16777232 | tf_op jit(solution)/shard_map/all_gather | solution.py:42
  292.8 20.0 %fusion = bf16[1,768,1024]{1,2,0:T(8,128)(2,1)} fusion(bf16[8192,1024]{1,0:T(8,128)(2,1)} %all-gather.4.cloned.1.call-done, bf16[768,8192]{1,0:T(8,128)(2,1)} %all-gather.6.cloned.1.call-done), kind=kOutput, calls=%fused_computation.9 | convolution fusion | flops 12885688320 | bytes 30932992 | tf_op jit(solution)/shard_map/dot_general | solution.py:40
  312.8 106.8 %all-gather.8.cloned.1.call-done = bf16[8192,1024]{1,0:T(8,128)(2,1)} async-done(((bf16[512,1024]{1,0:T(8,128)(2,1)}), bf16[8192,1024]{1,0:T(8,128)(2,1)}) %all-gather.8.cloned.1.call-update) | async-done | bytes 16777232 | tf_op jit(solution)/shard_map/all_gather | solution.py:42
  419.7 0.0 copy-start.1
  419.7 19.0 %fusion.1 = bf16[1,768,1024]{1,2,0:T(8,128)(2,1)S(1)} fusion(bf16[8192,1024]{1,0:T(8,128)(2,1)} %all-gather.8.cloned.1.call-done, bf16[768,8192]{1,0:T(8,128)(2,1)} %all-gather.6.cloned.1.call-done), kind=kOutput, calls=%fused_computation.10 | convolution fusion | flops 12885688320 | bytes 30932992 | tf_op jit(solution)/shard_map/dot_general | solution.py:40
  438.7 0.0 copy-done.1
  438.7 0.3 pad_maximum_fusion
  439.0 2.9 copy.6
  (3 shorter events, 0.0 us)
Async XLA Ops:
  6.5 0.9 copy-start.2
  6.5 1.0 copy-start.3
  6.5 157.6 %all-gather.6.cloned.1.call-start = ((), (), s32[]{:S(2)}) async-start(), calls=%async_computation.1 | async-start | bytes 18874368 | tf_op jit(solution)/shard_map/all_gather | solution.py:30
  7.3 285.6 %all-gather.4.cloned.1.call-start = ((), (), s32[]{:S(2)}) async-start(), calls=%async_computation | async-start | bytes 17825792 | tf_op jit(solution)/shard_map/all_gather | solution.py:42
  7.5 1.9 copy-start
  9.4 37.7 %copy-start.4 = (f32[2,1024]{1,0:T(2,128)S(1)}, f32[2,1024]{1,0:T(2,128)}, u32[]{:S(2)}) copy-start(f32[2,1024]{1,0:T(2,128)} %param.9) | copy-start | bytes 24580
  50.1 369.6 %all-gather.8.cloned.1.call-start = ((), (), s32[]{:S(2)}) async-start(), calls=%async_computation.2 | async-start | bytes 17825792 | tf_op jit(solution)/shard_map/all_gather | solution.py:42
  419.7 19.0 %copy-start.1 = (bf16[1,768,1024]{1,2,0:T(8,128)(2,1)S(1)}, bf16[1,768,1024]{1,2,0:T(8,128)(2,1)}, u32[]{:S(2)}) copy-start(bf16[1,768,1024]{1,2,0:T(8,128)(2,1)} %fusion) | copy-start | bytes 4718596
Sparse Core Ops, SparseCore 0:
  8.9 155.2 all-gather.5
  166.4 126.4 all-gather.3
  295.0 124.5 all-gather.7
where the time goes:
time: 449 us; the launch traced here: 448 us
  waiting for transfers between devices  349 us (78%)
  matrix products  42.7 us (10%)
  blocking collectives  35.9 us (8%)
  between operations  13.2 us (3%)
    all_gather x2, waiting for transfers between devices, local(): lax.all_gather(prefilled_key_values, ('dp', 'rep'), axis=0, tiled=True)  235 us
    all_gather x1, waiting for transfers between devices, local(): features = lax.all_gather(prompts, 'tp', axis=1, tiled=True)  113 us
    dot_general x2, matrix products, local(): jnp.dot(features, lax.all_gather(prefilled_key_values, ('dp', 'rep'), axi...  39 us
    psum x1, blocking collectives, prefilled_shard_values(): lax.psum(jnp.sum(combined_weight * combined_weight, axis=0), ('dp', 'rep'))  35.9 us
  transfers between devices with their start and end apart: 3, of which 3 were waited for; matrix products, arithmetic and copies ran while one was open for 6% of the time, Pallas kernels for 0%

commit v1 on v0

v1 whole, which is shorter than its diff:
```python
import functools

import jax
import jax.numpy as jnp
from jax import lax
from jax.experimental import pallas as pl
from jax.experimental.pallas import tpu as pltpu
from jax.sharding import PartitionSpec as P

epsilon = 1e-06
MESH = pl.DeviceIdType.MESH


def merge_rows(weight_rows, down_rows, up_matrix):
    return weight_rows.astype(jnp.float32) + jnp.einsum(
        "lrk,lkc->lrc", down_rows, up_matrix, preferred_element_type=jnp.float32
    )


def kernel(
    sizes, prompts_ref, merged_ref, magnitude_ref, out_ref,
    wbuf, pbuf, acc, squares,
    arrive, zsend, zown, ysend, csend, psend, parrive, load_p, load_w,
):
    tp_size, dp_size, rep_size = sizes
    y_size = dp_size // 2
    layers, rows, columns = merged_ref.shape
    groups = dp_size // tp_size
    x = lax.axis_index("tp")
    d = lax.axis_index("dp")
    z = lax.axis_index("rep")
    y, c = d // 2, lax.rem(d, 2)
    partner = {"tp": x, "dp": d + 1 - 2 * c, "rep": z}

    pieces = [(0, 0, rows // 4), (0, rows // 4, rows - rows // 4)]
    for layer in range(1, layers):
        pieces += [(layer, 0, rows // 2), (layer, rows // 2, rows // 2)]
    count = len(pieces)

    def block(yy, cc, zz):
        return (yy * 2 + cc) * rep_size + zz

    def piece(b, s):
        layer, start, size = pieces[s]
        return wbuf.at[b, layer, pl.ds(start, size), :]

    pending = []

    def send(cond, ref, send_sem, recv_sem, device):
        def make():
            return pltpu.make_async_remote_copy(
                src_ref=ref, dst_ref=ref, send_sem=send_sem, recv_sem=recv_sem,
                device_id=device, device_id_type=MESH,
            )

        pending.append((cond, make))
        if cond is None:
            make().start()
        else:
            @pl.when(cond)
            def _():
                make().start()

    def wait_piece(b, s):
        pltpu.make_async_remote_copy(
            src_ref=piece(b, s), dst_ref=piece(b, s), send_sem=csend.at[0],
            recv_sem=arrive.at[b * count + s], device_id=partner, device_id_type=MESH,
        ).wait_recv()

    def z_device(step):
        return {"tp": x, "dp": d, "rep": z + step}

    def y_device(o):
        return {"tp": x, "dp": lax.rem(y + o, y_size) * 2 + c, "rep": z}

    def to_partner(cond, yy, zz, s):
        b = block(yy, c, zz)
        send(cond, piece(b, s), csend.at[(yy * rep_size + zz) * count + s], arrive.at[b * count + s], partner)

    def to_y(cond, zz, s):
        b = block(y, c, zz)
        for o in range(1, y_size):
            send(
                cond, piece(b, s), ysend.at[((o - 1) * rep_size + zz) * count + s],
                arrive.at[b * count + s], y_device(o),
            )

    def along_z(cond, yy, zz, s, step):
        b = block(yy, c, zz)
        send(
            cond, piece(b, s), zsend.at[(yy * rep_size + zz) * count + s],
            arrive.at[b * count + s], z_device(step),
        )

    def start_z(yy, s):
        b = block(yy, c, z)
        send(z < rep_size - 1, piece(b, s), zown.at[yy * count + s], arrive.at[b * count + s], z_device(1))
        along_z(z > 0, yy, z, s, -1)

    def when(cond, body):
        if cond is None:
            body()
        else:
            pl.when(cond)(body)

    me = block(y, c, z)
    load_weight = pltpu.make_async_copy(merged_ref, wbuf.at[me], load_w)
    load_weight.start()

    table = [sorted(range(rep_size), key=lambda k: (abs(k - at), k)) for at in range(rep_size)]

    def nearest(i):
        value = jnp.int32(table[0][i])
        for at in range(1, rep_size):
            value = jnp.where(z == at, jnp.int32(table[at][i]), value)
        return value

    own_chunks = []
    for i in range(rep_size):
        for g in range(groups):
            own_chunks.append((g * rep_size + nearest(i), x * groups * rep_size + g * rep_size + nearest(i)))

    def load_chunk(j, b):
        start = pl.multiple_of(j * rows, rows)
        return pltpu.make_async_copy(prompts_ref.at[:, pl.ds(start, rows)], pbuf.at[b], load_p.at[b])

    for j, b in own_chunks:
        load_chunk(j, b).start()

    barrier = pltpu.get_barrier_semaphore()
    pl.semaphore_signal(barrier, 1, device_id=partner, device_id_type=MESH)
    for o in range(1, y_size):
        pl.semaphore_signal(barrier, 1, device_id=y_device(o), device_id_type=MESH)
    for o in range(1, tp_size):
        pl.semaphore_signal(
            barrier, 1, device_id={"tp": lax.rem(x + o, tp_size), "dp": d, "rep": z}, device_id_type=MESH
        )

    @pl.when(z > 0)
    def _():
        pl.semaphore_signal(barrier, 1, device_id=z_device(-1), device_id_type=MESH)

    @pl.when(z < rep_size - 1)
    def _():
        pl.semaphore_signal(barrier, 1, device_id=z_device(1), device_id_type=MESH)

    neighbours = jnp.where(z > 0, 1, 0) + jnp.where(z < rep_size - 1, 1, 0)
    pl.semaphore_wait(barrier, neighbours + (1 + y_size - 1 + tp_size - 1))

    load_weight.wait()
    for s in range(count):
        to_y(None, z, s)
        start_z(y, s)
    for j, b in own_chunks:
        load_chunk(j, b).wait()
        for o in range(1, tp_size):
            send(
                None, pbuf.at[b], psend.at[(o - 1) * dp_size * rep_size + b], parrive.at[b],
                {"tp": lax.rem(x + o, tp_size), "dp": d, "rep": z},
            )
    for s in range(count):
        to_partner(None, y, z, s)

    acc[...] = jnp.zeros_like(acc)
    squares[...] = jnp.zeros_like(squares)
    tile = min(256, columns)

    def wait_chunk(b):
        @pl.when(b // (groups * rep_size) != x)
        def _():
            pltpu.make_async_remote_copy(
                src_ref=pbuf.at[b], dst_ref=pbuf.at[b], send_sem=psend.at[0], recv_sem=parrive.at[b],
                device_id=partner, device_id_type=MESH,
            ).wait_recv()

    def compute(b, first, last):
        tiles = columns // tile

        def step(t, carry):
            layer = first + t // tiles
            at = pl.ds(pl.multiple_of(lax.rem(t, tiles) * tile, tile), tile)
            weight = wbuf[b, layer, :, at]
            acc[layer, :, at] += jnp.dot(pbuf[b], weight, preferred_element_type=jnp.float32)
            wide = weight.astype(jnp.float32)
            squares[layer, :, at] += jnp.sum((wide * wide).reshape(rows // 8, 8, tile), axis=0)
            return carry

        lax.fori_loop(0, (last - first) * tiles, step, 0)

    def finish(zz):
        mine, other = block(y, c, zz), block(y, 1 - c, zz)
        wait_chunk(mine)
        compute(mine, 0, layers)
        for s in range(count):
            wait_piece(other, s)
        wait_chunk(other)
        compute(other, 0, layers)
        for o in range(1, y_size):
            yy = lax.rem(y + o, y_size)
            mine, other = block(yy, c, zz), block(yy, 1 - c, zz)
            for layer in range(layers):
                held = [s for s in range(count) if pieces[s][0] == layer]
                for s in held:
                    if s > 0:
                        wait_piece(mine, s)
                        to_partner_plain(yy, zz, s)
                if layer == 0:
                    wait_chunk(mine)
                compute(mine, layer, layer + 1)
                for s in held:
                    wait_piece(other, s)
                if layer == 0:
                    wait_chunk(other)
                compute(other, layer, layer + 1)

    def to_partner_plain(yy, zz, s):
        b = block(yy, c, zz)

        def make():
            return pltpu.make_async_remote_copy(
                src_ref=piece(b, s), dst_ref=piece(b, s), send_sem=csend.at[(yy * rep_size + zz) * count + s],
                recv_sem=arrive.at[b * count + s], device_id=partner, device_id_type=MESH,
            )

        make().start()

    def take(zz, s, step):
        onward = (z + step >= 0) & (z + step <= rep_size - 1)

        def arrived(yy):
            b = block(yy, c, zz)
            wait_piece(b, s)

            @pl.when(onward)
            def _():
                pltpu.make_async_remote_copy(
                    src_ref=piece(b, s), dst_ref=piece(b, s), send_sem=zsend.at[(yy * rep_size + zz) * count + s],
                    recv_sem=arrive.at[b * count + s], device_id=z_device(step), device_id_type=MESH,
                ).start()

        arrived(y)
        if s > 0:
            b = block(y, c, zz)
            for o in range(1, y_size):
                pltpu.make_async_remote_copy(
                    src_ref=piece(b, s), dst_ref=piece(b, s),
                    send_sem=ysend.at[((o - 1) * rep_size + zz) * count + s],
                    recv_sem=arrive.at[b * count + s], device_id=y_device(o), device_id_type=MESH,
                ).start()
        to_partner_plain(y, zz, s)
        if s == 0:
            for o in range(1, y_size):
                yy = lax.rem(y + o, y_size)
                arrived(yy)
                to_partner_plain(yy, zz, 0)

    for o in range(1, y_size):
        yy = lax.rem(y + o, y_size)
        wait_piece(block(yy, c, z), 0)
        start_z(yy, 0)
        to_partner(None, yy, z, 0)

    def sides(r):
        return ((z - r >= 0, z - r, 1), (z + r <= rep_size - 1, z + r, -1))

    for r in range(1, rep_size):
        for s in range(count):
            for valid, zz, step in sides(r):
                pl.when(valid)(functools.partial(take, zz, s, step))
        if r == 1:
            finish(z)
        else:
            for valid, zz, _ in sides(r - 1):
                pl.when(valid)(functools.partial(finish, zz))
    if rep_size == 1:
        finish(z)
    else:
        for valid, zz, _ in sides(rep_size - 1):
            pl.when(valid)(functools.partial(finish, zz))

    for layer in range(layers):
        total = jnp.sum(squares[layer], axis=0, keepdims=True)
        factor = magnitude_ref[pl.ds(layer, 1), :] / jnp.sqrt(total + epsilon)
        out_ref[layer] = (acc[layer] * factor).astype(out_ref.dtype)

    def drain(cond, make):
        when(cond, lambda: make().wait_send())

    for cond, make in pending:
        drain(cond, make)

    def sent(ref, sem):
        return pltpu.make_async_remote_copy(
            src_ref=ref, dst_ref=ref, send_sem=sem, recv_sem=arrive.at[0], device_id=partner, device_id_type=MESH
        )

    for r in range(1, rep_size):
        for valid, zz, step in sides(r):
            @pl.when(valid)
            def _(zz=zz, step=step):
                onward = (z + step >= 0) & (z + step <= rep_size - 1)
                for s in range(count):
                    for o in range(y_size):
                        yy = lax.rem(y + o, y_size)
                        at = (yy * rep_size + zz) * count + s
                        ref = piece(block(yy, c, zz), s)
                        sent(ref, csend.at[at]).wait_send()
                        if o == 0 or s == 0:
                            @pl.when(onward)
                            def _():
                                sent(ref, zsend.at[at]).wait_send()
                    if s > 0:
                        for o in range(1, y_size):
                            sent(
                                piece(block(y, c, zz), s), ysend.at[((o - 1) * rep_size + zz) * count + s]
                            ).wait_send()
    for o in range(1, y_size):
        yy = lax.rem(y + o, y_size)
        for s in range(1, count):
            sent(piece(block(yy, c, z), s), csend.at[(yy * rep_size + z) * count + s]).wait_send()


def local(sizes, prompts, frozen_projection_weight, lowrank_down_factor, lowrank_up_factor, magnitude):
    tp_size, dp_size, rep_size = sizes
    merged = merge_rows(frozen_projection_weight, lowrank_down_factor, lowrank_up_factor).astype(jnp.bfloat16)
    layers, rows, columns = merged.shape
    tokens = prompts.shape[0]
    blocks = dp_size * rep_size
    y_size = dp_size // 2
    count = 2 * layers
    dma = pltpu.SemaphoreType.DMA
    return pl.pallas_call(
        functools.partial(kernel, sizes),
        out_shape=jax.ShapeDtypeStruct((layers, tokens, columns), jnp.bfloat16),
        in_specs=[
            pl.BlockSpec(memory_space=pl.ANY),
            pl.BlockSpec(memory_space=pl.ANY),
            pl.BlockSpec(memory_space=pltpu.VMEM),
        ],
        out_specs=pl.BlockSpec(memory_space=pltpu.VMEM),
        scratch_shapes=[
            pltpu.VMEM((blocks, layers, rows, columns), jnp.bfloat16),
            pltpu.VMEM((blocks, tokens, rows), jnp.bfloat16),
            pltpu.VMEM((layers, tokens, columns), jnp.float32),
            pltpu.VMEM((layers, 8, columns), jnp.float32),
            dma((blocks * count,)),
            dma((y_size * rep_size * count,)),
            dma((y_size * count,)),
            dma((max(1, (y_size - 1) * rep_size * count),)),
            dma((y_size * rep_size * count,)),
            dma((max(1, (tp_size - 1) * blocks),)),
            dma((blocks,)),
            dma((blocks,)),
            dma(()),
        ],
        compiler_params=pltpu.CompilerParams(
            collective_id=0, has_side_effects=True, vmem_limit_bytes=66_000_000
        ),
        cost_estimate=pl.CostEstimate(
            flops=2 * layers * tokens * columns * rows * blocks, bytes_accessed=2 * blocks * rows * columns,
            transcendentals=0,
        ),
    )(prompts, merged, magnitude)


def solution(mesh):
    in_specs = (
        P(("dp", "rep"), "tp"),
        P(None, ("dp", "rep"), "tp"),
        P(None, ("dp", "rep"), None),
        P(None, None, "tp"),
        P(None, "tp"),
    )
    out_specs = P(None, ("dp", "rep"), "tp")
    sizes = tuple(mesh.shape[name] for name in ("tp", "dp", "rep"))
    return jax.shard_map(
        functools.partial(local, sizes), mesh=mesh, in_specs=in_specs, out_specs=out_specs, check_vma=False
    )
```

time: 449 us -> 200 us (0.45)
  waiting for transfers between devices: 349 us -> 0 us
  Pallas kernels: 0 us -> 191 us
  matrix products: 42.7 us -> 3.74 us
  blocking collectives: 35.9 us -> 0 us
  between operations: 13.2 us -> 0.01 us
    all_gather x3 -> x0, waiting for transfers between devices: 348 us -> none  [the longest x2 235 us: local(): lax.all_gather(prefilled_key_values, ('dp', 'rep'), axis=0, tiled=True)]
    pallas_call x0 -> x1, Pallas kernels: none -> 191 us  [local(): pl.pallas_call(functools.partial(kernel, sizes), out_shape=jax.ShapeDtype...]
    dot_general x4 -> x1, matrix products: 42.7 us -> 3.74 us  [merge_rows(): jnp.einsum('lrk,lkc->lrc', down_rows, up_matrix, preferred_element_type=j...]
    psum x1 -> x0, blocking collectives: 35.9 us -> none  [prefilled_shard_values(): lax.psum(jnp.sum(combined_weight * combined_weight, axis=0), ('dp', 'rep'))]
    unnamed x10 -> x3, local copies, waits for them, and re-layouts: 0.27 us -> 4.81 us
  transfers between devices with their start and end apart: 3 -> 0, of which waited for: 3 -> 0; matrix products, arithmetic and copies ran while one was open for 6% -> 0% of each run, Pallas kernels for 0% -> 0%
where the time goes in v1:
time: 200 us
  Pallas kernels  191 us (96%)
  local copies, waits for them, and re-layouts  4.81 us (2%)
  matrix products  3.74 us (2%)
    pallas_call x1, Pallas kernels, local(): pl.pallas_call(functools.partial(kernel, sizes), out_shape=jax.ShapeDtype...  191 us
    unnamed x3, local copies, waits for them, and re-layouts  4.81 us

profile of v1, /device:TPU:0, one launch (start us, length us, event | category | flops | bytes accessed | tf_op | source)
XLA Modules:
  0.0 199.7 jit_solution(1262789630093286211)
XLA Ops:
  0.0 0.0 copy-start
  0.0 0.9 copy-done
  1.0 3.7 %add_convert_fusion.merged_ref = bf16[2,512,1024]{2,1,0:T(8,128)(2,1)} fusion(bf16[2,512,1024]{2,1,0:T(8,128)(2,1)} %param.6, bf16[2,512,64]{1,2,0:T(8,128)(2,1)} %param.7, bf16[2,64,1024]{2,1,0:T(8,128)(2,1)S(1)} %copy-done), kind=kOutput, calls=%fused_computation | convolution fusion | flops 137363456 | bytes 4587520 | tf_op jit(solution)/shard_map/lrk,lkc->lrc/dot_general | solution.py:15
  4.7 191.1 %shard_map.55 = bf16[2,768,1024]{2,1,0:T(8,128)(2,1)} custom-call(bf16[768,4096]{1,0:T(8,128)(2,1)} %prompts_ref.1, bf16[2,512,1024]{2,1,0:T(8,128)(2,1)} %add_convert_fusion.merged_ref, f32[2,1024]{1,0:T(2,128)} %magnitude_ref.1), custom_call_target="tpu_custom_call" | custom-call | flops 25769803776 | bytes 16777216 | tf_op jit(solution)/shard_map/pallas_call | solution.py:332
  195.8 3.9 %copy.7 = bf16[2,768,1024]{2,1,0:T(8,128)(2,1)} copy(bf16[2,768,1024]{2,1,0:T(8,128)(2,1)} %shard_map.55) | data formatting | bytes 6291456
Async XLA Ops:
  0.0 1.0 copy-start

commit v2 on v1

--- a/solution.py
+++ b/solution.py
@@ -18,8 +18,8 @@
 
 
 def kernel(
-    sizes, prompts_ref, merged_ref, magnitude_ref, out_ref,
-    wbuf, pbuf, acc, squares,
+    sizes, prompts_ref, merged_ref, acc, squares,
+    wbuf, pbuf,
     arrive, zsend, zown, ysend, csend, psend, parrive, load_p, load_w,
 ):
     tp_size, dp_size, rep_size = sizes
@@ -32,7 +32,8 @@
     y, c = d // 2, lax.rem(d, 2)
     partner = {"tp": x, "dp": d + 1 - 2 * c, "rep": z}
 
-    pieces = [(0, 0, rows // 4), (0, rows // 4, rows - rows // 4)]
+    early = rows * 5 // 16
+    pieces = [(0, 0, early), (0, early, rows - early)]
     for layer in range(1, layers):
         pieces += [(layer, 0, rows // 2), (layer, rows // 2, rows // 2)]
     count = len(pieces)
@@ -187,7 +188,21 @@
 
         lax.fori_loop(0, (last - first) * tiles, step, 0)
 
-    def finish(zz):
+    def held(layer):
+        return [s for s in range(count) if pieces[s][0] == layer]
+
+    def own_layer(zz, layer):
+        mine, other = block(y, c, zz), block(y, 1 - c, zz)
+        if layer == 0:
+            wait_chunk(mine)
+        compute(mine, layer, layer + 1)
+        for s in held(layer):
+            wait_piece(other, s)
+        if layer == 0:
+            wait_chunk(other)
+        compute(other, layer, layer + 1)
+
+    def own(zz):
         mine, other = block(y, c, zz), block(y, 1 - c, zz)
         wait_chunk(mine)
         compute(mine, 0, layers)
@@ -195,19 +210,20 @@
             wait_piece(other, s)
         wait_chunk(other)
         compute(other, 0, layers)
+
+    def across(zz):
         for o in range(1, y_size):
             yy = lax.rem(y + o, y_size)
             mine, other = block(yy, c, zz), block(yy, 1 - c, zz)
             for layer in range(layers):
-                held = [s for s in range(count) if pieces[s][0] == layer]
-                for s in held:
+                for s in held(layer):
                     if s > 0:
                         wait_piece(mine, s)
                         to_partner_plain(yy, zz, s)
                 if layer == 0:
                     wait_chunk(mine)
                 compute(mine, layer, layer + 1)
-                for s in held:
+                for s in held(layer):
                     wait_piece(other, s)
                 if layer == 0:
                     wait_chunk(other)
@@ -263,25 +279,53 @@
     def sides(r):
         return ((z - r >= 0, z - r, 1), (z + r <= rep_size - 1, z + r, -1))
 
+    far = jnp.maximum(z, rep_size - 1 - z)
+
+    def each(r, cond, body):
+        def run():
+            if 2 * r <= rep_size - 1:
+                for valid, zz, step in sides(r):
+                    pl.when(valid)(functools.partial(body, zz, step))
+            else:
+                low = z - r >= 0
+                body(jnp.where(low, z - r, z + r), jnp.where(low, 1, -1))
+
+        pl.when(cond & (r <= far))(run)
+
+    def take_all(r, some):
+        for s in some:
+            each(r, r <= far, lambda zz, step, s=s: take(zz, s, step))
+
+    if rep_size > 1:
+        take_all(1, range(count))
+    own(z)
+    across(z)
+    if rep_size > 1:
+        each(1, far == 1, lambda zz, step: own(zz))
+    for r in range(2, rep_size):
+        two = (z - (r - 1) >= 0) & (z + (r - 1) <= rep_size - 1)
+        one = jnp.logical_not(two) & (r <= far)
+        last = r == far
+        take_all(r, range(2))
+        each(r - 1, one, lambda zz, step: own(zz))
+        take_all(r, range(2, count - 1))
+        each(r - 1, one, lambda zz, step: across(zz))
+        each(r, one & last, lambda zz, step: own_layer(zz, 0))
+        take_all(r, range(count - 1, count))
+
+        def rest(zz, step):
+            for layer in range(1, layers):
+                own_layer(zz, layer)
+
+        each(r, one & last, rest)
+        if 2 * (r - 1) <= rep_size - 1:
+            both = two & (r <= far)
+            each(r - 1, both, lambda zz, step: own(zz))
+            each(r, both & last, lambda zz, step: own(zz))
+            each(r - 1, both, lambda zz, step: across(zz))
     for r in range(1, rep_size):
-        for s in range(count):
-            for valid, zz, step in sides(r):
-                pl.when(valid)(functools.partial(take, zz, s, step))
-        if r == 1:
-            finish(z)
-        else:
-            for valid, zz, _ in sides(r - 1):
-                pl.when(valid)(functools.partial(finish, zz))
-    if rep_size == 1:
-        finish(z)
-    else:
-        for valid, zz, _ in sides(rep_size - 1):
-            pl.when(valid)(functools.partial(finish, zz))
-
-    for layer in range(layers):
-        total = jnp.sum(squares[layer], axis=0, keepdims=True)
-        factor = magnitude_ref[pl.ds(layer, 1), :] / jnp.sqrt(total + epsilon)
-        out_ref[layer] = (acc[layer] * factor).astype(out_ref.dtype)
+        if any(max(at, rep_size - 1 - at) == r for at in range(rep_size)):
+            each(r, far == r, lambda zz, step: across(zz))
 
     def drain(cond, make):
         when(cond, lambda: make().wait_send())
@@ -329,20 +373,20 @@
     y_size = dp_size // 2
     count = 2 * layers
     dma = pltpu.SemaphoreType.DMA
-    return pl.pallas_call(
+    product, squares = pl.pallas_call(
         functools.partial(kernel, sizes),
-        out_shape=jax.ShapeDtypeStruct((layers, tokens, columns), jnp.bfloat16),
+        out_shape=(
+            jax.ShapeDtypeStruct((layers, tokens, columns), jnp.float32),
+            jax.ShapeDtypeStruct((layers, 8, columns), jnp.float32),
+        ),
         in_specs=[
             pl.BlockSpec(memory_space=pl.ANY),
             pl.BlockSpec(memory_space=pl.ANY),
-            pl.BlockSpec(memory_space=pltpu.VMEM),
         ],
-        out_specs=pl.BlockSpec(memory_space=pltpu.VMEM),
+        out_specs=(pl.BlockSpec(memory_space=pltpu.VMEM), pl.BlockSpec(memory_space=pltpu.VMEM)),
         scratch_shapes=[
             pltpu.VMEM((blocks, layers, rows, columns), jnp.bfloat16),
             pltpu.VMEM((blocks, tokens, rows), jnp.bfloat16),
-            pltpu.VMEM((layers, tokens, columns), jnp.float32),
-            pltpu.VMEM((layers, 8, columns), jnp.float32),
             dma((blocks * count,)),
             dma((y_size * rep_size * count,)),
             dma((y_size * count,)),
@@ -360,7 +404,9 @@
             flops=2 * layers * tokens * columns * rows * blocks, bytes_accessed=2 * blocks * rows * columns,
             transcendentals=0,
         ),
-    )(prompts, merged, magnitude)
+    )(prompts, merged)
+    factor = magnitude / jnp.sqrt(jnp.sum(squares, axis=1) + epsilon)
+    return (product * factor[:, None, :]).astype(jnp.bfloat16)
 
 
 def solution(mesh):

time: 200 us -> 199 us (level)
  other arithmetic: 0 us -> 6.27 us
  local copies, waits for them, and re-layouts: 4.81 us -> 0.95 us
  Pallas kernels: 191 us -> 188 us
    convert_element_type x0 -> x1, other arithmetic: none -> 5.39 us  [local(): return (product * factor[:, None, :]).astype(jnp.bfloat16)]
    unnamed x3 -> x4, local copies, waits for them, and re-layouts: 4.81 us -> 0.95 us
    pallas_call x1, Pallas kernels: 191 us -> 188 us  [local(): pl.pallas_call(functools.partial(kernel, sizes), out_shape=(jax.ShapeDtyp...]
where the time goes in v2:
time: 199 us
  Pallas kernels  188 us (94%)
  other arithmetic  6.27 us (3%)
  matrix products  3.74 us (2%)
    pallas_call x1, Pallas kernels, local(): pl.pallas_call(functools.partial(kernel, sizes), out_shape=(jax.ShapeDtyp...  188 us
    convert_element_type x1, other arithmetic, local(): return (product * factor[:, None, :]).astype(jnp.bfloat16)  5.39 us

profile of v2, /device:TPU:0, one launch (start us, length us, event | category | flops | bytes accessed | tf_op | source)
XLA Modules:
  0.0 198.7 jit_solution(313526172988800252)
XLA Ops:
  0.0 0.0 copy-start
  0.0 0.9 copy-done
  1.0 3.7 %add_convert_fusion.merged_ref = bf16[2,512,1024]{2,1,0:T(8,128)(2,1)} fusion(bf16[2,512,1024]{2,1,0:T(8,128)(2,1)} %param.6, bf16[2,512,64]{1,2,0:T(8,128)(2,1)} %param.7, bf16[2,64,1024]{2,1,0:T(8,128)(2,1)S(1)} %copy-done), kind=kOutput, calls=%fused_computation.1 | convolution fusion | flops 137363456 | bytes 4587520 | tf_op jit(solution)/shard_map/lrk,lkc->lrc/dot_general | solution.py:15
  4.7 0.0 copy-start.1
  4.7 187.7 %shard_map.55 = (f32[2,768,1024]{2,1,0:T(8,128)}, f32[2,8,1024]{2,1,0:T(8,128)}) custom-call(bf16[768,4096]{1,0:T(8,128)(2,1)} %prompts_ref.1, bf16[2,512,1024]{2,1,0:T(8,128)(2,1)} %add_convert_fusion.merged_ref), custom_call_target="tpu_custom_call" | custom-call | flops 25769803776 | bytes 16777216 | tf_op jit(solution)/shard_map/pallas_call | solution.py:376
  192.4 0.9 reduce_sum.9
  193.3 0.0 copy-done.1
  193.3 5.4 %multiply_convert_fusion = bf16[2,768,1024]{2,1,0:T(8,128)(2,1)} fusion(f32[2,768,1024]{2,1,0:T(8,128)} %get-tuple-element.7, f32[2,1024]{1,0:T(2,128)S(1)} %rsqrt_multiply_fusion), kind=kLoop, calls=%fused_computation | loop fusion | flops 3145728 | bytes 9445376 | tf_op jit(solution)/shard_map/convert_element_type | solution.py:409
  (1 shorter events, 0.0 us)
Async XLA Ops:
  0.0 1.0 copy-start
  4.7 188.6 %copy-start.1 = (f32[2,1024]{1,0:T(2,128)S(1)}, f32[2,1024]{1,0:T(2,128)}, u32[]{:S(2)}) copy-start(f32[2,1024]{1,0:T(2,128)} %param.9) | copy-start | bytes 24580
